TPU v7x, 256 devices: a whole 4x4x8 slice. The times are simulated.
256 devices in a mesh: row: 64 (over z_hi, y, x, core), col: 4 (over z_lo).
Axes of the slice: x: 4, y: 4, z: 8 (z_hi: 2, z_lo: 4; z = z_hi * 4 + z_lo), core: 2. Of those that a mesh axis runs over, the one named last changes fastest.
Arguments:
- species: float32 [4, 512, 256, 256], P(None, None, 'row', 'col'), may hold values from -6 to 6
- symbol_x: float32 [512], replicated, may hold values from 0.3 to 3
- symbol_y: float32 [256], replicated, may hold values from 0.3 to 3
- symbol_z: float32 [256], replicated, may hold values from 0.3 to 3
Outputs:
- coefficients: float32 [4, 512, 256, 256], P(None, 'row', 'col')
All inputs are finite; a program needn't handle non-finite values.
Results may differ from a plain program's by a relative error of at most 0.00007.
Values sent between devices are 32-bit elements; how exact they have to be, the bound alone decides.
A program may use at most 64 MiB of HBM per device.

v0:
```python
import functools

import jax
import jax.numpy as jnp
import ml_dtypes
import numpy as np
from jax import lax
from jax.experimental import pallas as pl
from jax.experimental.pallas import tpu as pltpu
from jax.sharding import PartitionSpec as P

MESH = pl.DeviceIdType.MESH


def transform_table(count):
    rank = np.arange(count)
    step = (rank[:, None] + 1) * (rank[None, :] + 1) % (2 * count + 2)
    table = (np.sin(np.pi / (count + 1) * step) * (2.0 / (count + 1)) ** 0.5).astype(np.float32)
    return table


def halves_of(table):
    high = table.astype(ml_dtypes.bfloat16)
    low = (table - high.astype(np.float32)).astype(ml_dtypes.bfloat16)
    return np.stack([high, low])


def split(values):
    high = values.astype(jnp.bfloat16)
    return high, (values - high.astype(jnp.float32)).astype(jnp.bfloat16)


def product(left, right, dims):
    dot = functools.partial(
        lax.dot_general, dimension_numbers=(dims, ((), ())), preferred_element_type=jnp.float32
    )
    return dot(left[0], right[0]) + (dot(left[0], right[1]) + dot(left[1], right[0]))


def kernel(
    rows, cols,
    field, table_x, table_y, table_z, symbol_x, symbol_y, symbol_z,
    out,
    x_out, y_in, y_out, z_in,
    send_a, recv_a, send_b, recv_b,
):
    fields = field.shape[0]
    row, col = lax.axis_index("row"), lax.axis_index("col")
    share_x = x_out.shape[2]
    share_k = z_in.shape[3]
    pairs = z_in.shape[2]
    lane = lax.broadcasted_iota(jnp.int32, (1, 128), 1)
    low_half = lane < 64

    def join(first, second):
        return (
            jnp.where(low_half, first, pltpu.roll(second, 64, 1)),
            jnp.where(low_half, pltpu.roll(first, 64, 1), second),
        )

    barrier = pltpu.get_barrier_semaphore()

    def greet_row(at, carry):
        pl.semaphore_signal(barrier, inc=1, device_id=(row ^ at, col), device_id_type=MESH)
        return carry

    def greet_col(at, carry):
        pl.semaphore_signal(barrier, inc=1, device_id=(row, col ^ at), device_id_type=MESH)
        return carry

    lax.fori_loop(1, rows, greet_row, 0)
    lax.fori_loop(1, cols, greet_col, 0)

    def stage_x(f, carry):
        modes = product(
            (table_x[0], table_x[1]), split(field[f]), (((1,), (1,)))
        )
        x_out[f] = modes.reshape(x_out.shape[1:])
        y_in[f, row] = x_out[f, row]

        @pl.when(f == 0)
        def _():
            pl.semaphore_wait(barrier, rows + cols - 2)

        def send(at, carry):
            peer = row ^ at
            pltpu.make_async_remote_copy(
                x_out.at[f, peer], y_in.at[f, row], send_a.at[f], recv_a.at[f],
                device_id=(peer, col), device_id_type=MESH,
            ).start()
            return carry

        lax.fori_loop(1, rows, send, 0)
        return carry

    lax.fori_loop(0, fields, stage_x, 0)

    def stage_y(f, carry):
        others = y_in.at[f, pl.ds(0, rows - 1)]
        pltpu.make_async_copy(others, others, recv_a.at[f]).wait()
        columns = []
        for pair in range(pairs):
            even = y_in[f, :, 2 * pair, :]
            odd = y_in[f, :, 2 * pair + 1, :]
            planes = join(even[:, :128], odd[:, :128]) + join(even[:, 128:], odd[:, 128:])
            columns.append(jnp.concatenate(planes, axis=0))
        lines = jnp.concatenate(columns, axis=1)
        modes = product((table_y[0], table_y[1]), split(lines), (((1,), (0,))))
        for pair in range(pairs):
            block = modes[:, 128 * pair : 128 * (pair + 1)].reshape(cols, share_k, 128)
            for at in range(cols):
                y_out[f, at, pair] = block[at]
        z_in[f, col] = y_out[f, col]

        def send(at, carry):
            peer = col ^ at
            pltpu.make_async_remote_copy(
                y_out.at[f, peer], z_in.at[f, col], send_b.at[f], recv_b.at[f],
                device_id=(row, peer), device_id_type=MESH,
            ).start()
            return carry

        lax.fori_loop(1, cols, send, 0)
        return carry

    lax.fori_loop(0, fields, stage_y, 0)

    here = lax.broadcasted_iota(jnp.int32, (share_k, 256), 0) + col * share_k
    there = lax.broadcasted_iota(jnp.int32, (share_k, 256), 1)
    part_y = jnp.sum(jnp.where(here == there, symbol_y[...], 0.0), axis=1, keepdims=True)
    symbol_yz = part_y + symbol_z[...]

    def stage_z(f, carry):
        others = z_in.at[f, pl.ds(0, cols - 1)]
        pltpu.make_async_copy(others, others, recv_b.at[f]).wait()
        lines = []
        for pair in range(pairs):
            even0, odd0 = join(z_in[f, 0, pair], z_in[f, 1, pair])
            even1, odd1 = join(z_in[f, 2, pair], z_in[f, 3, pair])
            lines.append(jnp.concatenate([even0, even1], axis=1))
            lines.append(jnp.concatenate([odd0, odd1], axis=1))
        lines = jnp.concatenate(lines, axis=0)
        modes = product(split(lines), (table_z[0], table_z[1]), (((1,), (0,))))
        for x in range(share_x):
            symbol = symbol_yz + symbol_x[row * share_x + x]
            out[f, x] = modes[share_k * x : share_k * (x + 1)] / symbol
        return carry

    lax.fori_loop(0, fields, stage_z, 0)

    def drain(f, carry):
        sent = x_out.at[f, pl.ds(0, rows - 1)]
        pltpu.make_async_copy(sent, sent, send_a.at[f]).wait()
        sent = y_out.at[f, pl.ds(0, cols - 1)]
        pltpu.make_async_copy(sent, sent, send_b.at[f]).wait()
        return carry

    lax.fori_loop(0, fields, drain, 0)


def on_device(rows, cols, tables, species, symbol_x, symbol_y, symbol_z):
    fields, grid_x, share_y, share_z = species.shape
    grid_y, grid_z = share_y * rows, share_z * cols
    share_x, share_k = grid_x // rows, grid_y // cols
    field = species.transpose(0, 2, 3, 1).reshape(fields, share_y * share_z, grid_x)
    vmem = pl.BlockSpec(memory_space=pltpu.VMEM)
    smem = pl.BlockSpec(memory_space=pltpu.SMEM)
    return pl.pallas_call(
        functools.partial(kernel, rows, cols),
        out_shape=jax.ShapeDtypeStruct((fields, share_x, share_k, grid_z), jnp.float32),
        in_specs=[vmem, vmem, vmem, vmem, smem, vmem, vmem],
        out_specs=vmem,
        scratch_shapes=[
            pltpu.VMEM((fields, rows, share_x, share_y * share_z), jnp.float32),
            pltpu.VMEM((fields, rows, share_x, share_y * share_z), jnp.float32),
            pltpu.VMEM((fields, cols, share_x // 2, share_k, 2 * share_z), jnp.float32),
            pltpu.VMEM((fields, cols, share_x // 2, share_k, 2 * share_z), jnp.float32),
            pltpu.SemaphoreType.DMA((fields,)),
            pltpu.SemaphoreType.DMA((fields,)),
            pltpu.SemaphoreType.DMA((fields,)),
            pltpu.SemaphoreType.DMA((fields,)),
        ],
        compiler_params=pltpu.CompilerParams(
            collective_id=0, has_side_effects=True, vmem_limit_bytes=60 * 2**20
        ),
    )(field, *tables, symbol_x, symbol_y[None], symbol_z[None])


def solution(mesh):
    rows, cols = mesh.shape["row"], mesh.shape["col"]

    def whole(species, symbol_x, symbol_y, symbol_z):
        _, grid_x, grid_y, grid_z = species.shape
        share_y = grid_y // rows
        order = np.arange(grid_y).reshape(rows, share_y).T.reshape(-1)
        tables = (
            jnp.asarray(halves_of(transform_table(grid_x))),
            jnp.asarray(halves_of(transform_table(grid_y)[:, order])),
            jnp.asarray(halves_of(transform_table(grid_z))),
        )
        return jax.shard_map(
            functools.partial(on_device, rows, cols),
            mesh=mesh,
            in_specs=((P(), P(), P()), P(None, None, "row", "col"), P(), P(), P()),
            out_specs=P(None, "row", "col", None),
            check_vma=False,
        )(tables, species, symbol_x, symbol_y, symbol_z)

    return whole
```

profile of v0, /device:TPU:33, one launch (start us, length us, event | category | flops | bytes accessed | tf_op | source)
XLA Modules:
  0.0 110.8 jit_solution(11116040321354779420)
XLA Ops:
  0.0 107.7 %shard_map.73 = f32[4,8,64,256]{3,2,1,0:T(8,128)} custom-call(f32[4,256,512]{2,1,0:T(8,128)} %bitcast.5, bf16[2,512,512]{2,1,0:T(8,128)(2,1)} %constant.6.clone.table_x, bf16[2,256,256]{2,1,0:T(8,128)(2,1)} %constant.7.clone.table_y, bf16[2,256,256]{2,1,0:T(8,128)(2,1)} %constant.8.clone.table_z, f32[512]{0:T(512)} %symbol_x.1, f32[1,256]{1,0:T(1,128)} %bitcast.6, ...), custom_call_target="tpu_custom_call" | custom-call | tf_op jit(solution)/shard_map/pallas_call | solution.py:168
  107.7 3.1 %copy.9 = f32[4,8,64,256]{3,2,1,0:T(8,128)} copy(f32[4,8,64,256]{3,2,1,0:T(8,128)} %shard_map.73) | data formatting | bytes 4194304
where the time goes:
time: 111 us
  Pallas kernels  108 us (97%)
  local copies, waits for them, and re-layouts  3.13 us (3%)
    pallas_call x1, Pallas kernels, on_device(): pl.pallas_call(functools.partial(kernel, rows, cols), out_shape=jax.Shape...  108 us
    unnamed x1, local copies, waits for them, and re-layouts  3.13 us

commit v1 on v0

--- a/solution.py
+++ b/solution.py
@@ -39,16 +39,50 @@
 
 def kernel(
     rows, cols,
+    field_hbm, table_x_hbm, table_y_hbm, table_z_hbm, symbol_x_hbm, symbol_y_hbm, symbol_z_hbm,
+    out,
     field, table_x, table_y, table_z, symbol_x, symbol_y, symbol_z,
-    out,
-    x_out, y_in, y_out, z_in,
-    send_a, recv_a, send_b, recv_b,
+    x_out, middle, y_in, y_out, z_in,
+    send_m, recv_m, send_a, recv_a, send_b, recv_b, load_field, load_rest,
 ):
     fields = field.shape[0]
     row, col = lax.axis_index("row"), lax.axis_index("col")
     share_x = x_out.shape[2]
     share_k = z_in.shape[3]
     pairs = z_in.shape[2]
+
+    barrier = pltpu.get_barrier_semaphore()
+
+    half = rows // 2
+    partner = row ^ half
+    plane = row // half * half
+    place = row - plane
+
+    def greet_row(at, carry):
+        pl.semaphore_signal(barrier, inc=1, device_id=(row ^ at, col), device_id_type=MESH)
+        return carry
+
+    def greet_col(at, carry):
+        pl.semaphore_signal(barrier, inc=1, device_id=(row, col ^ at), device_id_type=MESH)
+        return carry
+
+    loads = [pltpu.make_async_copy(field_hbm.at[f], field.at[f], load_field.at[f]) for f in range(fields)]
+    rest = [
+        pltpu.make_async_copy(source, target, load_rest.at[at])
+        for at, (source, target) in enumerate((
+            (table_x_hbm, table_x), (table_y_hbm, table_y), (table_z_hbm, table_z),
+            (symbol_x_hbm, symbol_x), (symbol_y_hbm, symbol_y), (symbol_z_hbm, symbol_z),
+        ))
+    ]
+    loads[0].start()
+    rest[0].start()
+    pl.semaphore_signal(barrier, inc=1, device_id=(partner, col), device_id_type=MESH)
+    lax.fori_loop(1, half, greet_row, 0)
+    lax.fori_loop(1, cols, greet_col, 0)
+    for copy in loads[1:] + rest[1:]:
+        copy.start()
+    rest[0].wait()
+
     lane = lax.broadcasted_iota(jnp.int32, (1, 128), 1)
     low_half = lane < 64
 
@@ -58,29 +92,17 @@
             jnp.where(low_half, pltpu.roll(first, 64, 1), second),
         )
 
-    barrier = pltpu.get_barrier_semaphore()
-
-    def greet_row(at, carry):
-        pl.semaphore_signal(barrier, inc=1, device_id=(row ^ at, col), device_id_type=MESH)
-        return carry
-
-    def greet_col(at, carry):
-        pl.semaphore_signal(barrier, inc=1, device_id=(row, col ^ at), device_id_type=MESH)
-        return carry
-
-    lax.fori_loop(1, rows, greet_row, 0)
-    lax.fori_loop(1, cols, greet_col, 0)
-
-    def stage_x(f, carry):
-        modes = product(
-            (table_x[0], table_x[1]), split(field[f]), (((1,), (1,)))
-        )
+    def compute_x(f):
+        pltpu.make_async_copy(field_hbm.at[f], field.at[f], load_field.at[f]).wait()
+        modes = product((table_x[0], table_x[1]), split(field[f]), (((1,), (1,))))
         x_out[f] = modes.reshape(x_out.shape[1:])
         y_in[f, row] = x_out[f, row]
 
-        @pl.when(f == 0)
-        def _():
-            pl.semaphore_wait(barrier, rows + cols - 2)
+    def send_x(f):
+        pltpu.make_async_remote_copy(
+            x_out.at[f, pl.ds(half - plane, half)], middle.at[f], send_m.at[f], recv_m.at[f],
+            device_id=(partner, col), device_id_type=MESH,
+        ).start()
 
         def send(at, carry):
             peer = row ^ at
@@ -90,13 +112,24 @@
             ).start()
             return carry
 
-        lax.fori_loop(1, rows, send, 0)
-        return carry
-
-    lax.fori_loop(0, fields, stage_x, 0)
-
-    def stage_y(f, carry):
-        others = y_in.at[f, pl.ds(0, rows - 1)]
+        lax.fori_loop(1, half, send, 0)
+
+    def pass_on(f):
+        pltpu.make_async_copy(middle.at[f], middle.at[f], recv_m.at[f]).wait()
+
+        def send(at, carry):
+            peer = row ^ at
+            pltpu.make_async_remote_copy(
+                middle.at[f, place ^ at], y_in.at[f, partner], send_a.at[f], recv_a.at[f],
+                device_id=(peer, col), device_id_type=MESH,
+            ).start()
+            return carry
+
+        lax.fori_loop(1, half, send, 0)
+        y_in[f, partner] = middle[f, place]
+
+    def stage_y(f):
+        others = y_in.at[f, pl.ds(0, rows - 2)]
         pltpu.make_async_copy(others, others, recv_a.at[f]).wait()
         columns = []
         for pair in range(pairs):
@@ -121,14 +154,33 @@
             return carry
 
         lax.fori_loop(1, cols, send, 0)
-        return carry
-
-    lax.fori_loop(0, fields, stage_y, 0)
+
+    def first(f, carry):
+        compute_x(f)
+
+        @pl.when(f == 0)
+        def _():
+            pl.semaphore_wait(barrier, half + cols - 1)
+
+        send_x(f)
+        return carry
+
+    lax.fori_loop(0, fields, first, 0)
+    for copy in rest[1:]:
+        copy.wait()
+
+    def second(f, carry):
+        pass_on(f)
+        stage_y(f)
+        return carry
+
+    lax.fori_loop(0, fields, second, 0)
 
     here = lax.broadcasted_iota(jnp.int32, (share_k, 256), 0) + col * share_k
     there = lax.broadcasted_iota(jnp.int32, (share_k, 256), 1)
     part_y = jnp.sum(jnp.where(here == there, symbol_y[...], 0.0), axis=1, keepdims=True)
     symbol_yz = part_y + symbol_z[...]
+    at_x = lax.broadcasted_iota(jnp.int32, symbol_x.shape, 1) - row * share_x
 
     def stage_z(f, carry):
         others = z_in.at[f, pl.ds(0, cols - 1)]
@@ -142,14 +194,15 @@
         lines = jnp.concatenate(lines, axis=0)
         modes = product(split(lines), (table_z[0], table_z[1]), (((1,), (0,))))
         for x in range(share_x):
-            symbol = symbol_yz + symbol_x[row * share_x + x]
-            out[f, x] = modes[share_k * x : share_k * (x + 1)] / symbol
+            part_x = jnp.sum(jnp.where(at_x == x, symbol_x[...], 0.0), axis=1, keepdims=True)
+            out[f, x] = modes[share_k * x : share_k * (x + 1)] / (part_x + symbol_yz)
         return carry
 
     lax.fori_loop(0, fields, stage_z, 0)
 
     def drain(f, carry):
-        sent = x_out.at[f, pl.ds(0, rows - 1)]
+        pltpu.make_async_copy(middle.at[f], middle.at[f], send_m.at[f]).wait()
+        sent = x_out.at[f, pl.ds(0, rows - 2)]
         pltpu.make_async_copy(sent, sent, send_a.at[f]).wait()
         sent = y_out.at[f, pl.ds(0, cols - 1)]
         pltpu.make_async_copy(sent, sent, send_b.at[f]).wait()
@@ -163,15 +216,20 @@
     grid_y, grid_z = share_y * rows, share_z * cols
     share_x, share_k = grid_x // rows, grid_y // cols
     field = species.transpose(0, 2, 3, 1).reshape(fields, share_y * share_z, grid_x)
-    vmem = pl.BlockSpec(memory_space=pltpu.VMEM)
-    smem = pl.BlockSpec(memory_space=pltpu.SMEM)
+    hbm = pl.BlockSpec(memory_space=pltpu.HBM)
     return pl.pallas_call(
         functools.partial(kernel, rows, cols),
-        out_shape=jax.ShapeDtypeStruct((fields, share_x, share_k, grid_z), jnp.float32),
-        in_specs=[vmem, vmem, vmem, vmem, smem, vmem, vmem],
-        out_specs=vmem,
+        out_shape=pltpu.VMEM((fields, share_x, share_k, grid_z), jnp.float32),
+        in_specs=[hbm] * 7,
+        out_specs=pl.BlockSpec(memory_space=pltpu.VMEM),
         scratch_shapes=[
+            pltpu.VMEM(field.shape, jnp.float32),
+            *(pltpu.VMEM(table.shape, table.dtype) for table in tables),
+            pltpu.VMEM((1, grid_x), jnp.float32),
+            pltpu.VMEM((1, grid_y), jnp.float32),
+            pltpu.VMEM((1, grid_z), jnp.float32),
             pltpu.VMEM((fields, rows, share_x, share_y * share_z), jnp.float32),
+            pltpu.VMEM((fields, rows // 2, share_x, share_y * share_z), jnp.float32),
             pltpu.VMEM((fields, rows, share_x, share_y * share_z), jnp.float32),
             pltpu.VMEM((fields, cols, share_x // 2, share_k, 2 * share_z), jnp.float32),
             pltpu.VMEM((fields, cols, share_x // 2, share_k, 2 * share_z), jnp.float32),
@@ -179,11 +237,15 @@
             pltpu.SemaphoreType.DMA((fields,)),
             pltpu.SemaphoreType.DMA((fields,)),
             pltpu.SemaphoreType.DMA((fields,)),
+            pltpu.SemaphoreType.DMA((fields,)),
+            pltpu.SemaphoreType.DMA((fields,)),
+            pltpu.SemaphoreType.DMA((fields,)),
+            pltpu.SemaphoreType.DMA((6,)),
         ],
         compiler_params=pltpu.CompilerParams(
-            collective_id=0, has_side_effects=True, vmem_limit_bytes=60 * 2**20
+            collective_id=0, has_side_effects=True, vmem_limit_bytes=20 * 2**20
         ),
-    )(field, *tables, symbol_x, symbol_y[None], symbol_z[None])
+    )(*(pltpu.with_memory_space_constraint(a, pltpu.HBM) for a in (field, *tables, symbol_x[None], symbol_y[None], symbol_z[None])))
 
 
 def solution(mesh):

time: 111 us -> 103 us (0.928)
  Pallas kernels: 108 us -> 101 us
  local copies, waits for them, and re-layouts: 3.13 us -> 1.32 us
    pallas_call x1, Pallas kernels: 108 us -> 101 us  [on_device(): pl.pallas_call(functools.partial(kernel, rows, cols), out_shape=pltpu.VME...]
    unnamed x1, local copies, waits for them, and re-layouts: 3.13 us -> 1.32 us
where the time goes in v1:
time: 103 us
  Pallas kernels  101 us (98%)
  local copies, waits for them, and re-layouts  1.32 us (1%)
    pallas_call x1, Pallas kernels, on_device(): pl.pallas_call(functools.partial(kernel, rows, cols), out_shape=pltpu.VME...  101 us

profile of v1, /device:TPU:33, one launch (start us, length us, event | category | flops | bytes accessed | tf_op | source)
XLA Modules:
  0.0 102.6 jit_solution(6985812340901266879)
XLA Ops:
  0.0 101.3 %shard_map.73 = f32[4,8,64,256]{3,2,1,0:T(8,128)S(1)} custom-call(f32[4,256,512]{2,1,0:T(8,128)} %bitcast.6, bf16[2,512,512]{2,1,0:T(8,128)(2,1)} %constant.6.clone.table_x_hbm, bf16[2,256,256]{2,1,0:T(8,128)(2,1)} %constant.7.clone.table_y_hbm, bf16[2,256,256]{2,1,0:T(8,128)(2,1)} %constant.8.clone.table_z_hbm, f32[1,512]{1,0:T(1,128)} %bitcast.7, ...), custom_call_target="tpu_custom_call" | custom-call | tf_op jit(solution)/shard_map/pallas_call | solution.py:220
  101.3 1.3 %copy.9 = f32[4,8,64,256]{3,2,1,0:T(8,128)} copy(f32[4,8,64,256]{3,2,1,0:T(8,128)S(1)} %shard_map.73) | data formatting | bytes 4194304

commit v2 on v1

--- a/solution.py
+++ b/solution.py
@@ -1,4 +1,5 @@
 import functools
+import math
 
 import jax
 import jax.numpy as jnp
@@ -42,8 +43,8 @@
     field_hbm, table_x_hbm, table_y_hbm, table_z_hbm, symbol_x_hbm, symbol_y_hbm, symbol_z_hbm,
     out,
     field, table_x, table_y, table_z, symbol_x, symbol_y, symbol_z,
-    x_out, middle, y_in, y_out, z_in,
-    send_m, recv_m, send_a, recv_a, send_b, recv_b, load_field, load_rest,
+    x_out, relay, middle, y_in, y_out, z_in,
+    token, send_r, recv_r, send_w, send_m, recv_m, send_a, recv_a, send_b, recv_b, load_field, load_rest,
 ):
     fields = field.shape[0]
     row, col = lax.axis_index("row"), lax.axis_index("col")
@@ -57,14 +58,24 @@
     partner = row ^ half
     plane = row // half * half
     place = row - plane
-
-    def greet_row(at, carry):
-        pl.semaphore_signal(barrier, inc=1, device_id=(row ^ at, col), device_id_type=MESH)
-        return carry
-
-    def greet_col(at, carry):
-        pl.semaphore_signal(barrier, inc=1, device_id=(row, col ^ at), device_id_type=MESH)
-        return carry
+    side = math.isqrt(half // 2)
+    layers = 2 * cols
+    layer = row // half * cols + col
+    at_x, at_y = lax.rem(place // 2, side), place // (2 * side)
+
+    def ring(step):
+        there = lax.rem(layer + step + layers, layers)
+        return place + there // cols * half, lax.rem(there, cols)
+
+    def beside_x(step):
+        return row + 2 * (lax.rem(at_x + step + side, side) - at_x), col
+
+    def beside_y(step):
+        return row + 2 * side * (lax.rem(at_y + step + side, side) - at_y), col
+
+    def signal(semaphore, *devices):
+        for device in devices:
+            pl.semaphore_signal(semaphore, inc=1, device_id=device, device_id_type=MESH)
 
     loads = [pltpu.make_async_copy(field_hbm.at[f], field.at[f], load_field.at[f]) for f in range(fields)]
     rest = [
@@ -74,12 +85,16 @@
             (symbol_x_hbm, symbol_x), (symbol_y_hbm, symbol_y), (symbol_z_hbm, symbol_z),
         ))
     ]
-    loads[0].start()
+    straight, relayed = range(fields // 2), range(fields // 2, fields)
+    loads[relayed[0]].start()
     rest[0].start()
-    pl.semaphore_signal(barrier, inc=1, device_id=(partner, col), device_id_type=MESH)
-    lax.fori_loop(1, half, greet_row, 0)
-    lax.fori_loop(1, cols, greet_col, 0)
-    for copy in loads[1:] + rest[1:]:
+    signal(
+        barrier, ring(1), ring(-1), (row ^ 1, col),
+        beside_x(1), beside_x(-1), beside_y(1), beside_y(-1),
+    )
+    for f in (*relayed[1:], *straight):
+        loads[f].start()
+    for copy in rest[1:]:
         copy.start()
     rest[0].wait()
 
@@ -98,12 +113,27 @@
         x_out[f] = modes.reshape(x_out.shape[1:])
         y_in[f, row] = x_out[f, row]
 
-    def send_x(f):
-        pltpu.make_async_remote_copy(
+    def relay_of(f, way):
+        return pltpu.make_async_remote_copy(
+            x_out.at[f, pl.ds(half - plane + way * (half // 2), half // 2)],
+            relay.at[f - relayed[0], way], send_r.at[f - relayed[0], way], recv_r.at[f - relayed[0], way],
+            device_id=ring(1 - 2 * way), device_id_type=MESH,
+        )
+
+    def forward_of(f, way):
+        return pltpu.make_async_remote_copy(
+            relay.at[f - relayed[0], way], middle.at[f, pl.ds(way * (half // 2), half // 2)],
+            send_w.at[f - relayed[0], way], recv_m.at[f],
+            device_id=ring(3 - 6 * way), device_id_type=MESH,
+        )
+
+    def across(f):
+        return pltpu.make_async_remote_copy(
             x_out.at[f, pl.ds(half - plane, half)], middle.at[f], send_m.at[f], recv_m.at[f],
             device_id=(partner, col), device_id_type=MESH,
-        ).start()
-
+        )
+
+    def send_x(f, carry):
         def send(at, carry):
             peer = row ^ at
             pltpu.make_async_remote_copy(
@@ -112,7 +142,7 @@
             ).start()
             return carry
 
-        lax.fori_loop(1, half, send, 0)
+        return lax.fori_loop(1, half, send, carry)
 
     def pass_on(f):
         pltpu.make_async_copy(middle.at[f], middle.at[f], recv_m.at[f]).wait()
@@ -155,17 +185,36 @@
 
         lax.fori_loop(1, cols, send, 0)
 
-    def first(f, carry):
-        compute_x(f)
-
-        @pl.when(f == 0)
-        def _():
-            pl.semaphore_wait(barrier, half + cols - 1)
-
-        send_x(f)
-        return carry
-
-    lax.fori_loop(0, fields, first, 0)
+    compute_x(relayed[0])
+    pl.semaphore_wait(barrier, 7)
+    relay_of(relayed[0], 0).start()
+    relay_of(relayed[0], 1).start()
+    signal(token.at[0], ring(1), ring(-1))
+    signal(token.at[1], beside_x(1), beside_x(-1))
+    compute_x(relayed[1])
+    relay_of(relayed[1], 0).start()
+    relay_of(relayed[1], 1).start()
+    pl.semaphore_wait(token.at[0], 2)
+    pl.semaphore_wait(token.at[1], 2)
+    signal(token.at[2], ring(1), ring(-1))
+    signal(token.at[3], beside_x(-1))
+    compute_x(straight[0])
+    pl.semaphore_wait(token.at[2], 2)
+    pl.semaphore_wait(token.at[3], 1)
+    signal(token.at[4], ring(1))
+    signal(token.at[5], beside_y(1), beside_y(-1))
+    compute_x(straight[1])
+    pl.semaphore_wait(token.at[4], 1)
+    for f in straight:
+        across(f).start()
+    pl.semaphore_wait(token.at[5], 2)
+    signal(token.at[6], beside_y(-1))
+    pl.semaphore_wait(token.at[6], 1)
+    lax.fori_loop(0, fields, send_x, 0)
+    for f in relayed:
+        for way in range(2):
+            relay_of(f, way).wait_recv()
+            forward_of(f, way).start()
     for copy in rest[1:]:
         copy.wait()
 
@@ -180,7 +229,7 @@
     there = lax.broadcasted_iota(jnp.int32, (share_k, 256), 1)
     part_y = jnp.sum(jnp.where(here == there, symbol_y[...], 0.0), axis=1, keepdims=True)
     symbol_yz = part_y + symbol_z[...]
-    at_x = lax.broadcasted_iota(jnp.int32, symbol_x.shape, 1) - row * share_x
+    lane_x = lax.broadcasted_iota(jnp.int32, symbol_x.shape, 1) - row * share_x
 
     def stage_z(f, carry):
         others = z_in.at[f, pl.ds(0, cols - 1)]
@@ -194,14 +243,13 @@
         lines = jnp.concatenate(lines, axis=0)
         modes = product(split(lines), (table_z[0], table_z[1]), (((1,), (0,))))
         for x in range(share_x):
-            part_x = jnp.sum(jnp.where(at_x == x, symbol_x[...], 0.0), axis=1, keepdims=True)
+            part_x = jnp.sum(jnp.where(lane_x == x, symbol_x[...], 0.0), axis=1, keepdims=True)
             out[f, x] = modes[share_k * x : share_k * (x + 1)] / (part_x + symbol_yz)
         return carry
 
     lax.fori_loop(0, fields, stage_z, 0)
 
     def drain(f, carry):
-        pltpu.make_async_copy(middle.at[f], middle.at[f], send_m.at[f]).wait()
         sent = x_out.at[f, pl.ds(0, rows - 2)]
         pltpu.make_async_copy(sent, sent, send_a.at[f]).wait()
         sent = y_out.at[f, pl.ds(0, cols - 1)]
@@ -209,6 +257,12 @@
         return carry
 
     lax.fori_loop(0, fields, drain, 0)
+    for f in straight:
+        across(f).wait_send()
+    for f in relayed:
+        for way in range(2):
+            relay_of(f, way).wait_send()
+            forward_of(f, way).wait_send()
 
 
 def on_device(rows, cols, tables, species, symbol_x, symbol_y, symbol_z):
@@ -229,10 +283,15 @@
             pltpu.VMEM((1, grid_y), jnp.float32),
             pltpu.VMEM((1, grid_z), jnp.float32),
             pltpu.VMEM((fields, rows, share_x, share_y * share_z), jnp.float32),
+            pltpu.VMEM((fields // 2, 2, rows // 4, share_x, share_y * share_z), jnp.float32),
             pltpu.VMEM((fields, rows // 2, share_x, share_y * share_z), jnp.float32),
             pltpu.VMEM((fields, rows, share_x, share_y * share_z), jnp.float32),
             pltpu.VMEM((fields, cols, share_x // 2, share_k, 2 * share_z), jnp.float32),
             pltpu.VMEM((fields, cols, share_x // 2, share_k, 2 * share_z), jnp.float32),
+            pltpu.SemaphoreType.REGULAR((7,)),
+            pltpu.SemaphoreType.DMA((fields // 2, 2)),
+            pltpu.SemaphoreType.DMA((fields // 2, 2)),
+            pltpu.SemaphoreType.DMA((fields // 2, 2)),
             pltpu.SemaphoreType.DMA((fields,)),
             pltpu.SemaphoreType.DMA((fields,)),
             pltpu.SemaphoreType.DMA((fields,)),

time: 103 us -> 99.9 us (0.970)
  Pallas kernels: 101 us -> 98.5 us
    pallas_call x1, Pallas kernels: 101 us -> 98.5 us  [on_device(): pl.pallas_call(functools.partial(kernel, rows, cols), out_shape=pltpu.VME...]
where the time goes in v2:
time: 99.9 us; the launch traced here: 99.8 us
  Pallas kernels  98.5 us (99%)
  local copies, waits for them, and re-layouts  1.32 us (1%)
    pallas_call x1, Pallas kernels, on_device(): pl.pallas_call(functools.partial(kernel, rows, cols), out_shape=pltpu.VME...  98.5 us

profile of v2, /device:TPU:33, one launch (start us, length us, event | category | flops | bytes accessed | tf_op | source)
XLA Modules:
  0.0 99.8 jit_solution(8878190835919375879)
XLA Ops:
  0.0 98.5 %shard_map.73 = f32[4,8,64,256]{3,2,1,0:T(8,128)S(1)} custom-call(f32[4,256,512]{2,1,0:T(8,128)} %bitcast.6, bf16[2,512,512]{2,1,0:T(8,128)(2,1)} %constant.6.clone.table_x_hbm, bf16[2,256,256]{2,1,0:T(8,128)(2,1)} %constant.7.clone.table_y_hbm, bf16[2,256,256]{2,1,0:T(8,128)(2,1)} %constant.8.clone.table_z_hbm, f32[1,512]{1,0:T(1,128)} %bitcast.7, ...), custom_call_target="tpu_custom_call" | custom-call | tf_op jit(solution)/shard_map/pallas_call | solution.py:274
  98.5 1.3 %copy.9 = f32[4,8,64,256]{3,2,1,0:T(8,128)} copy(f32[4,8,64,256]{3,2,1,0:T(8,128)S(1)} %shard_map.73) | data formatting | bytes 4194304

commit v3 on v2

--- a/solution.py
+++ b/solution.py
@@ -44,7 +44,7 @@
     out,
     field, table_x, table_y, table_z, symbol_x, symbol_y, symbol_z,
     x_out, relay, middle, y_in, y_out, z_in,
-    token, send_r, recv_r, send_w, send_m, recv_m, send_a, recv_a, send_b, recv_b, load_field, load_rest,
+    token, send_r, recv_r, send_w, recv_m, send_a, recv_a, send_b, recv_b, load_field, load_rest,
 ):
     fields = field.shape[0]
     row, col = lax.axis_index("row"), lax.axis_index("col")
@@ -85,16 +85,13 @@
             (symbol_x_hbm, symbol_x), (symbol_y_hbm, symbol_y), (symbol_z_hbm, symbol_z),
         ))
     ]
-    straight, relayed = range(fields // 2), range(fields // 2, fields)
-    loads[relayed[0]].start()
+    loads[0].start()
     rest[0].start()
     signal(
         barrier, ring(1), ring(-1), (row ^ 1, col),
         beside_x(1), beside_x(-1), beside_y(1), beside_y(-1),
     )
-    for f in (*relayed[1:], *straight):
-        loads[f].start()
-    for copy in rest[1:]:
+    for copy in loads[1:] + rest[1:]:
         copy.start()
     rest[0].wait()
 
@@ -116,21 +113,15 @@
     def relay_of(f, way):
         return pltpu.make_async_remote_copy(
             x_out.at[f, pl.ds(half - plane + way * (half // 2), half // 2)],
-            relay.at[f - relayed[0], way], send_r.at[f - relayed[0], way], recv_r.at[f - relayed[0], way],
+            relay.at[f, way], send_r.at[f, way], recv_r.at[f, way],
             device_id=ring(1 - 2 * way), device_id_type=MESH,
         )
 
     def forward_of(f, way):
         return pltpu.make_async_remote_copy(
-            relay.at[f - relayed[0], way], middle.at[f, pl.ds(way * (half // 2), half // 2)],
-            send_w.at[f - relayed[0], way], recv_m.at[f],
+            relay.at[f, way], middle.at[f, pl.ds(way * (half // 2), half // 2)],
+            send_w.at[f, way], recv_m.at[f],
             device_id=ring(3 - 6 * way), device_id_type=MESH,
-        )
-
-    def across(f):
-        return pltpu.make_async_remote_copy(
-            x_out.at[f, pl.ds(half - plane, half)], middle.at[f], send_m.at[f], recv_m.at[f],
-            device_id=(partner, col), device_id_type=MESH,
         )
 
     def send_x(f, carry):
@@ -185,33 +176,32 @@
 
         lax.fori_loop(1, cols, send, 0)
 
-    compute_x(relayed[0])
+    def prepare(f):
+        compute_x(f)
+        relay_of(f, 0).start()
+        relay_of(f, 1).start()
+
+    compute_x(0)
     pl.semaphore_wait(barrier, 7)
-    relay_of(relayed[0], 0).start()
-    relay_of(relayed[0], 1).start()
+    relay_of(0, 0).start()
+    relay_of(0, 1).start()
     signal(token.at[0], ring(1), ring(-1))
     signal(token.at[1], beside_x(1), beside_x(-1))
-    compute_x(relayed[1])
-    relay_of(relayed[1], 0).start()
-    relay_of(relayed[1], 1).start()
+    prepare(1)
     pl.semaphore_wait(token.at[0], 2)
     pl.semaphore_wait(token.at[1], 2)
     signal(token.at[2], ring(1), ring(-1))
     signal(token.at[3], beside_x(-1))
-    compute_x(straight[0])
+    prepare(2)
     pl.semaphore_wait(token.at[2], 2)
     pl.semaphore_wait(token.at[3], 1)
-    signal(token.at[4], ring(1))
-    signal(token.at[5], beside_y(1), beside_y(-1))
-    compute_x(straight[1])
-    pl.semaphore_wait(token.at[4], 1)
-    for f in straight:
-        across(f).start()
-    pl.semaphore_wait(token.at[5], 2)
-    signal(token.at[6], beside_y(-1))
-    pl.semaphore_wait(token.at[6], 1)
+    signal(token.at[4], beside_y(1), beside_y(-1))
+    prepare(3)
+    pl.semaphore_wait(token.at[4], 2)
+    signal(token.at[5], beside_y(-1))
+    pl.semaphore_wait(token.at[5], 1)
     lax.fori_loop(0, fields, send_x, 0)
-    for f in relayed:
+    for f in range(fields):
         for way in range(2):
             relay_of(f, way).wait_recv()
             forward_of(f, way).start()
@@ -257,9 +247,7 @@
         return carry
 
     lax.fori_loop(0, fields, drain, 0)
-    for f in straight:
-        across(f).wait_send()
-    for f in relayed:
+    for f in range(fields):
         for way in range(2):
             relay_of(f, way).wait_send()
             forward_of(f, way).wait_send()
@@ -283,16 +271,15 @@
             pltpu.VMEM((1, grid_y), jnp.float32),
             pltpu.VMEM((1, grid_z), jnp.float32),
             pltpu.VMEM((fields, rows, share_x, share_y * share_z), jnp.float32),
-            pltpu.VMEM((fields // 2, 2, rows // 4, share_x, share_y * share_z), jnp.float32),
+            pltpu.VMEM((fields, 2, rows // 4, share_x, share_y * share_z), jnp.float32),
             pltpu.VMEM((fields, rows // 2, share_x, share_y * share_z), jnp.float32),
             pltpu.VMEM((fields, rows, share_x, share_y * share_z), jnp.float32),
             pltpu.VMEM((fields, cols, share_x // 2, share_k, 2 * share_z), jnp.float32),
             pltpu.VMEM((fields, cols, share_x // 2, share_k, 2 * share_z), jnp.float32),
-            pltpu.SemaphoreType.REGULAR((7,)),
-            pltpu.SemaphoreType.DMA((fields // 2, 2)),
-            pltpu.SemaphoreType.DMA((fields // 2, 2)),
-            pltpu.SemaphoreType.DMA((fields // 2, 2)),
-            pltpu.SemaphoreType.DMA((fields,)),
+            pltpu.SemaphoreType.REGULAR((6,)),
+            pltpu.SemaphoreType.DMA((fields, 2)),
+            pltpu.SemaphoreType.DMA((fields, 2)),
+            pltpu.SemaphoreType.DMA((fields, 2)),
             pltpu.SemaphoreType.DMA((fields,)),
             pltpu.SemaphoreType.DMA((fields,)),
             pltpu.SemaphoreType.DMA((fields,)),

time: 99.9 us -> 97.6 us (0.977)
  Pallas kernels: 98.5 us -> 95.4 us
    pallas_call x1, Pallas kernels: 98.5 us -> 95.4 us  [on_device(): pl.pallas_call(functools.partial(kernel, rows, cols), out_shape=pltpu.VME...]
where the time goes in v3:
time: 97.6 us; the launch traced here: 96.7 us
  Pallas kernels  95.4 us (98%)
  local copies, waits for them, and re-layouts  1.32 us (1%)
    pallas_call x1, Pallas kernels, on_device(): pl.pallas_call(functools.partial(kernel, rows, cols), out_shape=pltpu.VME...  95.4 us

profile of v3, /device:TPU:33, one launch (start us, length us, event | category | flops | bytes accessed | tf_op | source)
XLA Modules:
  0.0 96.7 jit_solution(16134493887376198526)
XLA Ops:
  0.0 95.4 %shard_map.73 = f32[4,8,64,256]{3,2,1,0:T(8,128)S(1)} custom-call(f32[4,256,512]{2,1,0:T(8,128)} %bitcast.6, bf16[2,512,512]{2,1,0:T(8,128)(2,1)} %constant.6.clone.table_x_hbm, bf16[2,256,256]{2,1,0:T(8,128)(2,1)} %constant.7.clone.table_y_hbm, bf16[2,256,256]{2,1,0:T(8,128)(2,1)} %constant.8.clone.table_z_hbm, f32[1,512]{1,0:T(1,128)} %bitcast.7, ...), custom_call_target="tpu_custom_call" | custom-call | tf_op jit(solution)/shard_map/pallas_call | solution.py:262
  95.4 1.3 %copy.9 = f32[4,8,64,256]{3,2,1,0:T(8,128)} copy(f32[4,8,64,256]{3,2,1,0:T(8,128)S(1)} %shard_map.73) | data formatting | bytes 4194304

commit v4 on v3

--- a/solution.py
+++ b/solution.py
@@ -38,11 +38,50 @@
     return dot(left[0], right[0]) + (dot(left[0], right[1]) + dot(left[1], right[0]))
 
 
+def join(first, second):
+    low_half = lax.broadcasted_iota(jnp.int32, (1, 128), 1) < 64
+    return (
+        jnp.where(low_half, first, pltpu.roll(second, 64, 1)),
+        jnp.where(low_half, pltpu.roll(first, 64, 1), second),
+    )
+
+
+def modes_of_z(blocks, table_z, pairs):
+    lines = []
+    for pair in pairs:
+        even0, odd0 = join(blocks(0, pair), blocks(1, pair))
+        even1, odd1 = join(blocks(2, pair), blocks(3, pair))
+        lines.append(jnp.concatenate([even0, even1], axis=1))
+        lines.append(jnp.concatenate([odd0, odd1], axis=1))
+    lines = jnp.concatenate(lines, axis=0)
+    return product(split(lines), (table_z[0], table_z[1]), (((1,), (0,))))
+
+
+def finish(done, landed, table_z, symbol, out, staged, sems):
+    fields = done.shape[0]
+    share_x, share_k = symbol.shape[:2]
+    copies = [pltpu.make_async_copy(done.at[f], out.at[f], sems.at[f]) for f in range(fields)]
+    for copy in copies:
+        copy.start()
+    half = share_x // 2
+    for at in range(2):
+        modes = modes_of_z(
+            lambda c, pair: landed[c, pair], table_z, range(at * half // 2, (at + 1) * half // 2)
+        )
+        for x in range(half):
+            staged[at * half + x] = modes[share_k * x : share_k * (x + 1)] / symbol[at * half + x]
+        part = pl.ds(at * half, half)
+        copies.append(pltpu.make_async_copy(staged.at[part], out.at[fields, part], sems.at[fields + at]))
+        copies[-1].start()
+    for copy in copies:
+        copy.wait()
+
+
 def kernel(
     rows, cols,
     field_hbm, table_x_hbm, table_y_hbm, table_z_hbm, symbol_x_hbm, symbol_y_hbm, symbol_z_hbm,
-    out,
-    field, table_x, table_y, table_z, symbol_x, symbol_y, symbol_z,
+    out, landed, table_z, symbol,
+    field, table_x, table_y, symbol_x, symbol_y, symbol_z,
     x_out, relay, middle, y_in, y_out, z_in,
     token, send_r, recv_r, send_w, recv_m, send_a, recv_a, send_b, recv_b, load_field, load_rest,
 ):
@@ -94,15 +133,6 @@
     for copy in loads[1:] + rest[1:]:
         copy.start()
     rest[0].wait()
-
-    lane = lax.broadcasted_iota(jnp.int32, (1, 128), 1)
-    low_half = lane < 64
-
-    def join(first, second):
-        return (
-            jnp.where(low_half, first, pltpu.roll(second, 64, 1)),
-            jnp.where(low_half, pltpu.roll(first, 64, 1), second),
-        )
 
     def compute_x(f):
         pltpu.make_async_copy(field_hbm.at[f], field.at[f], load_field.at[f]).wait()
@@ -200,11 +230,11 @@
     pl.semaphore_wait(token.at[4], 2)
     signal(token.at[5], beside_y(-1))
     pl.semaphore_wait(token.at[5], 1)
-    lax.fori_loop(0, fields, send_x, 0)
     for f in range(fields):
         for way in range(2):
             relay_of(f, way).wait_recv()
             forward_of(f, way).start()
+    lax.fori_loop(0, fields, send_x, 0)
     for copy in rest[1:]:
         copy.wait()
 
@@ -220,24 +250,22 @@
     part_y = jnp.sum(jnp.where(here == there, symbol_y[...], 0.0), axis=1, keepdims=True)
     symbol_yz = part_y + symbol_z[...]
     lane_x = lax.broadcasted_iota(jnp.int32, symbol_x.shape, 1) - row * share_x
+    for x in range(share_x):
+        part_x = jnp.sum(jnp.where(lane_x == x, symbol_x[...], 0.0), axis=1, keepdims=True)
+        symbol[x] = part_x + symbol_yz
 
     def stage_z(f, carry):
         others = z_in.at[f, pl.ds(0, cols - 1)]
         pltpu.make_async_copy(others, others, recv_b.at[f]).wait()
-        lines = []
-        for pair in range(pairs):
-            even0, odd0 = join(z_in[f, 0, pair], z_in[f, 1, pair])
-            even1, odd1 = join(z_in[f, 2, pair], z_in[f, 3, pair])
-            lines.append(jnp.concatenate([even0, even1], axis=1))
-            lines.append(jnp.concatenate([odd0, odd1], axis=1))
-        lines = jnp.concatenate(lines, axis=0)
-        modes = product(split(lines), (table_z[0], table_z[1]), (((1,), (0,))))
+        modes = modes_of_z(lambda c, pair: z_in[f, c, pair], table_z, range(pairs))
         for x in range(share_x):
-            part_x = jnp.sum(jnp.where(lane_x == x, symbol_x[...], 0.0), axis=1, keepdims=True)
-            out[f, x] = modes[share_k * x : share_k * (x + 1)] / (part_x + symbol_yz)
+            out[f, x] = modes[share_k * x : share_k * (x + 1)] / symbol[x]
         return carry
 
-    lax.fori_loop(0, fields, stage_z, 0)
+    lax.fori_loop(0, fields - 1, stage_z, 0)
+    others = z_in.at[fields - 1, pl.ds(0, cols - 1)]
+    pltpu.make_async_copy(others, others, recv_b.at[fields - 1]).wait()
+    landed[...] = z_in[fields - 1]
 
     def drain(f, carry):
         sent = x_out.at[f, pl.ds(0, rows - 2)]
@@ -259,14 +287,19 @@
     share_x, share_k = grid_x // rows, grid_y // cols
     field = species.transpose(0, 2, 3, 1).reshape(fields, share_y * share_z, grid_x)
     hbm = pl.BlockSpec(memory_space=pltpu.HBM)
-    return pl.pallas_call(
+    done, landed, table_z, symbol = pl.pallas_call(
         functools.partial(kernel, rows, cols),
-        out_shape=pltpu.VMEM((fields, share_x, share_k, grid_z), jnp.float32),
+        out_shape=(
+            pltpu.VMEM((fields - 1, share_x, share_k, grid_z), jnp.float32),
+            pltpu.VMEM((cols, share_x // 2, share_k, 2 * share_z), jnp.float32),
+            pltpu.VMEM(tables[2].shape, tables[2].dtype),
+            pltpu.VMEM((share_x, share_k, grid_z), jnp.float32),
+        ),
         in_specs=[hbm] * 7,
-        out_specs=pl.BlockSpec(memory_space=pltpu.VMEM),
+        out_specs=(pl.BlockSpec(memory_space=pltpu.VMEM),) * 4,
         scratch_shapes=[
             pltpu.VMEM(field.shape, jnp.float32),
-            *(pltpu.VMEM(table.shape, table.dtype) for table in tables),
+            *(pltpu.VMEM(table.shape, table.dtype) for table in tables[:2]),
             pltpu.VMEM((1, grid_x), jnp.float32),
             pltpu.VMEM((1, grid_y), jnp.float32),
             pltpu.VMEM((1, grid_z), jnp.float32),
@@ -292,6 +325,18 @@
             collective_id=0, has_side_effects=True, vmem_limit_bytes=20 * 2**20
         ),
     )(*(pltpu.with_memory_space_constraint(a, pltpu.HBM) for a in (field, *tables, symbol_x[None], symbol_y[None], symbol_z[None])))
+    vmem = pl.BlockSpec(memory_space=pltpu.VMEM)
+    return pl.pallas_call(
+        finish,
+        out_shape=jax.ShapeDtypeStruct((fields, share_x, share_k, grid_z), jnp.float32),
+        in_specs=[vmem] * 4,
+        out_specs=pl.BlockSpec(memory_space=pltpu.HBM),
+        scratch_shapes=[
+            pltpu.VMEM((share_x, share_k, grid_z), jnp.float32),
+            pltpu.SemaphoreType.DMA((fields + 1,)),
+        ],
+        compiler_params=pltpu.CompilerParams(vmem_limit_bytes=8 * 2**20),
+    )(done, landed, table_z, symbol)
 
 
 def solution(mesh):

time: 97.6 us -> 97.3 us (level)
  local copies, waits for them, and re-layouts: 1.32 us -> 0 us
    unnamed x1 -> x0, local copies, waits for them, and re-layouts: 1.32 us -> none
    pallas_call x1 -> x2, Pallas kernels: 95.4 us -> 96.3 us  [the longest x1 95 us: on_device(): pl.pallas_call(functools.partial(kernel, rows, cols), out_shape=(pltpu.VM...]
where the time goes in v4:
time: 97.3 us; the launch traced here: 96.3 us
  Pallas kernels  96.3 us (99%)
    pallas_call x1, Pallas kernels, on_device(): pl.pallas_call(functools.partial(kernel, rows, cols), out_shape=(pltpu.VM...  95 us

profile of v4, /device:TPU:33, one launch (start us, length us, event | category | flops | bytes accessed | tf_op | source)
XLA Modules:
  0.0 96.3 jit_solution(16822394661270820452)
XLA Ops:
  0.0 95.0 %shard_map.73 = (f32[3,8,64,256]{3,2,1,0:T(8,128)S(1)}, f32[4,4,64,128]{3,2,1,0:T(8,128)S(1)}, bf16[2,256,256]{2,1,0:T(8,128)(2,1)S(1)}, f32[8,64,256]{2,1,0:T(8,128)S(1)}) custom-call(f32[4,256,512]{2,1,0:T(8,128)} %bitcast.6, bf16[2,512,512]{2,1,0:T(8,128)(2,1)} %constant.6.clone.table_x_hbm, bf16[2,256,256]{2,1,0:T(8,128)(2,1)} %constant.7.clone.table_y_hbm, ...), custom_call_target="tpu_custom_call" | custom-call | tf_op jit(solution)/shard_map/pallas_call | solution.py:290
  95.0 1.4 %shard_map.74 = f32[4,8,64,256]{3,2,1,0:T(8,128)} custom-call(f32[3,8,64,256]{3,2,1,0:T(8,128)S(1)} %get-tuple-element.9.done, f32[4,4,64,128]{3,2,1,0:T(8,128)S(1)} %get-tuple-element.10.landed, bf16[2,256,256]{2,1,0:T(8,128)(2,1)S(1)} %get-tuple-element.11.table_z, f32[8,64,256]{2,1,0:T(8,128)S(1)} %get-tuple-element.12.symbol), custom_call_target="tpu_custom_call" | custom-call | tf_op jit(solution)/shard_map/pallas_call | solution.py:329

commit v5 on v4

--- a/solution.py
+++ b/solution.py
@@ -127,9 +127,15 @@
     loads[0].start()
     rest[0].start()
     signal(
-        barrier, ring(1), ring(-1), (row ^ 1, col),
+        barrier, ring(1), ring(-1),
         beside_x(1), beside_x(-1), beside_y(1), beside_y(-1),
     )
+    core = lax.rem(place, 2)
+
+    @pl.when(core == 0)
+    def _():
+        signal(barrier, (row ^ 1, col))
+
     for copy in loads[1:] + rest[1:]:
         copy.start()
     rest[0].wait()
@@ -212,12 +218,22 @@
         relay_of(f, 1).start()
 
     compute_x(0)
-    pl.semaphore_wait(barrier, 7)
+    pl.semaphore_wait(barrier, 6 + core)
     relay_of(0, 0).start()
     relay_of(0, 1).start()
     signal(token.at[0], ring(1), ring(-1))
+
+    @pl.when(core == 1)
+    def _():
+        signal(token.at[6], (row ^ 1, col))
+
+    prepare(1)
+
+    @pl.when(core == 0)
+    def _():
+        pl.semaphore_wait(token.at[6], 1)
+
     signal(token.at[1], beside_x(1), beside_x(-1))
-    prepare(1)
     pl.semaphore_wait(token.at[0], 2)
     pl.semaphore_wait(token.at[1], 2)
     signal(token.at[2], ring(1), ring(-1))
@@ -229,11 +245,11 @@
     prepare(3)
     pl.semaphore_wait(token.at[4], 2)
     signal(token.at[5], beside_y(-1))
-    pl.semaphore_wait(token.at[5], 1)
     for f in range(fields):
         for way in range(2):
             relay_of(f, way).wait_recv()
             forward_of(f, way).start()
+    pl.semaphore_wait(token.at[5], 1)
     lax.fori_loop(0, fields, send_x, 0)
     for copy in rest[1:]:
         copy.wait()
@@ -309,7 +325,7 @@
             pltpu.VMEM((fields, rows, share_x, share_y * share_z), jnp.float32),
             pltpu.VMEM((fields, cols, share_x // 2, share_k, 2 * share_z), jnp.float32),
             pltpu.VMEM((fields, cols, share_x // 2, share_k, 2 * share_z), jnp.float32),
-            pltpu.SemaphoreType.REGULAR((6,)),
+            pltpu.SemaphoreType.REGULAR((7,)),
             pltpu.SemaphoreType.DMA((fields, 2)),
             pltpu.SemaphoreType.DMA((fields, 2)),
             pltpu.SemaphoreType.DMA((fields, 2)),

time: 97.3 us -> 97.3 us (level)
  no operation moved by 1% of the time
where the time goes in v5:
time: 97.3 us; the launch traced here: 96.4 us
  Pallas kernels  96.3 us (99%)
    pallas_call x1, Pallas kernels, on_device(): pl.pallas_call(functools.partial(kernel, rows, cols), out_shape=(pltpu.VM...  95 us

profile of v5, /device:TPU:33, one launch (start us, length us, event | category | flops | bytes accessed | tf_op | source)
XLA Modules:
  0.0 96.4 jit_solution(16800061778792343122)
XLA Ops:
  0.0 95.0 %shard_map.73 = (f32[3,8,64,256]{3,2,1,0:T(8,128)S(1)}, f32[4,4,64,128]{3,2,1,0:T(8,128)S(1)}, bf16[2,256,256]{2,1,0:T(8,128)(2,1)S(1)}, f32[8,64,256]{2,1,0:T(8,128)S(1)}) custom-call(f32[4,256,512]{2,1,0:T(8,128)} %bitcast.6, bf16[2,512,512]{2,1,0:T(8,128)(2,1)} %constant.6.clone.table_x_hbm, bf16[2,256,256]{2,1,0:T(8,128)(2,1)} %constant.7.clone.table_y_hbm, ...), custom_call_target="tpu_custom_call" | custom-call | tf_op jit(solution)/shard_map/pallas_call | solution.py:306
  95.0 1.4 %shard_map.74 = f32[4,8,64,256]{3,2,1,0:T(8,128)} custom-call(f32[3,8,64,256]{3,2,1,0:T(8,128)S(1)} %get-tuple-element.9.done, f32[4,4,64,128]{3,2,1,0:T(8,128)S(1)} %get-tuple-element.10.landed, bf16[2,256,256]{2,1,0:T(8,128)(2,1)S(1)} %get-tuple-element.11.table_z, f32[8,64,256]{2,1,0:T(8,128)S(1)} %get-tuple-element.12.symbol), custom_call_target="tpu_custom_call" | custom-call | tf_op jit(solution)/shard_map/pallas_call | solution.py:345

commit v6 on v5

--- a/solution.py
+++ b/solution.py
@@ -124,8 +124,6 @@
             (symbol_x_hbm, symbol_x), (symbol_y_hbm, symbol_y), (symbol_z_hbm, symbol_z),
         ))
     ]
-    loads[0].start()
-    rest[0].start()
     signal(
         barrier, ring(1), ring(-1),
         beside_x(1), beside_x(-1), beside_y(1), beside_y(-1),
@@ -136,7 +134,7 @@
     def _():
         signal(barrier, (row ^ 1, col))
 
-    for copy in loads[1:] + rest[1:]:
+    for copy in (loads[0], *rest[:1], *loads[1:], *rest[1:]):
         copy.start()
     rest[0].wait()
 

time: 97.3 us -> 97.3 us (level)
  no operation moved by 1% of the time
where the time goes in v6:
time: 97.3 us; the launch traced here: 96.4 us
  Pallas kernels  96.3 us (99%)
    pallas_call x1, Pallas kernels, on_device(): pl.pallas_call(functools.partial(kernel, rows, cols), out_shape=(pltpu.VM...  95 us

profile of v6, /device:TPU:33, one launch (start us, length us, event | category | flops | bytes accessed | tf_op | source)
XLA Modules:
  0.0 96.4 jit_solution(49165252984638576)
XLA Ops:
  0.0 95.0 %shard_map.73 = (f32[3,8,64,256]{3,2,1,0:T(8,128)S(1)}, f32[4,4,64,128]{3,2,1,0:T(8,128)S(1)}, bf16[2,256,256]{2,1,0:T(8,128)(2,1)S(1)}, f32[8,64,256]{2,1,0:T(8,128)S(1)}) custom-call(f32[4,256,512]{2,1,0:T(8,128)} %bitcast.6, bf16[2,512,512]{2,1,0:T(8,128)(2,1)} %constant.6.clone.table_x_hbm, bf16[2,256,256]{2,1,0:T(8,128)(2,1)} %constant.7.clone.table_y_hbm, ...), custom_call_target="tpu_custom_call" | custom-call | tf_op jit(solution)/shard_map/pallas_call | solution.py:304
  95.0 1.4 %shard_map.74 = f32[4,8,64,256]{3,2,1,0:T(8,128)} custom-call(f32[3,8,64,256]{3,2,1,0:T(8,128)S(1)} %get-tuple-element.9.done, f32[4,4,64,128]{3,2,1,0:T(8,128)S(1)} %get-tuple-element.10.landed, bf16[2,256,256]{2,1,0:T(8,128)(2,1)S(1)} %get-tuple-element.11.table_z, f32[8,64,256]{2,1,0:T(8,128)S(1)} %get-tuple-element.12.symbol), custom_call_target="tpu_custom_call" | custom-call | tf_op jit(solution)/shard_map/pallas_call | solution.py:343
